TPU v7x, 32 devices: a whole 2x2x4 slice. The times are simulated.
32 devices in a mesh: dp: 4 (over x, core), center: 8 (over z, y).
Axes of the slice: x: 2, y: 2, z: 4, core: 2. Of those that a mesh axis runs over, the one named last changes fastest.
Arguments:
- features: bfloat16 [4096, 1024], P('dp'), may hold values from -6 to 6
- centers: bfloat16 [4096, 1024], P('center'), may hold values from -6 to 6
- targets: bfloat16 [4096, 256], P('dp'), may hold values from -6 to 6
Outputs:
- coef: float32 [4096, 256], P('center')
- residual: float32 [4096, 256], P('center')
All inputs are finite; a program needn't handle non-finite values.
Results may differ from a plain program's by a relative error of at most 0.024.
Values may be sent and summed in bfloat16 or wider, within the bound.
No kernel may reach another device: no remote copies, remote signals or barrier semaphores. Data moves between devices by JAX's collectives and lax.ppermute only.
A program may use at most 64 MiB of HBM per device.

v0:
```python
import math
import jax
import jax.numpy as jnp
from jax import lax
from jax.sharding import PartitionSpec as P

BATCHES = 2
ITERS = 2


def kernel_block(rows, centers):
    scores = lax.dot_general(
        rows, centers, (((1,), (1,)), ((), ())), preferred_element_type=jnp.float32
    )
    lifted = 1.0 + 0.5 / math.sqrt(rows.shape[1]) * scores
    return (lifted * lifted * lifted).astype(jnp.bfloat16)


def build_kernel(features, centers):
    batch_rows = features.shape[0] // BATCHES
    pieces = [
        kernel_block(features[batch_index * batch_rows : (batch_index + 1) * batch_rows], centers)
        for batch_index in range(BATCHES)
    ]
    return jnp.concatenate(pieces, axis=0)


def transposed_sum(kernel, values):
    local = lax.dot_general(
        kernel, values, (((0,), (0,)), ((), ())), preferred_element_type=jnp.float32
    )
    return lax.psum(local, "dp")


def column_sums(values):
    return lax.psum(values, "center")


def whole_direction(direction):
    low_dir = direction.astype(jnp.bfloat16)
    return low_dir


def apply_operator(kernel, direction, total_rows):
    low_dir = whole_direction(direction)
    partial_value = jnp.dot(kernel, low_dir, preferred_element_type=jnp.float32)
    predicted = lax.psum(partial_value, "center").astype(jnp.bfloat16)
    return transposed_sum(kernel, predicted) / total_rows + 0.5 * direction


def on_device(features, centers, targets):
    total_rows = features.shape[0] * lax.axis_size("dp")
    kernel = build_kernel(features, centers)
    right_side = transposed_sum(kernel, targets) / math.sqrt(total_rows)
    coef = jnp.zeros_like(right_side)
    residual = right_side
    direction = right_side
    norm_now = column_sums(jnp.sum(residual * residual, axis=0))
    for turn in range(ITERS):
        image = apply_operator(kernel, direction, total_rows)
        curvature, mixed, image_sq = column_sums(
            (
                jnp.sum(direction * image, axis=0),
                jnp.sum(residual * image, axis=0),
                jnp.sum(image * image, axis=0),
            )
        )
        step_size = norm_now / (curvature + 1e-06)
        coef = coef + step_size * direction
        residual = residual - step_size * image
        if turn + 1 < ITERS:
            norm_next = norm_now - 2.0 * step_size * mixed + step_size * step_size * image_sq
            direction = residual + norm_next / (norm_now + 1e-06) * direction
            norm_now = norm_next
    return (coef, residual)


def solution(mesh):
    placed = (P("dp", None), P("center", None), P("dp", None))
    return jax.shard_map(
        on_device,
        mesh=mesh,
        in_specs=placed,
        out_specs=(P("center", None), P("center", None)),
        check_vma=False,
    )
```

profile of v0, /device:TPU:0, one launch (start us, length us, event | category | flops | bytes accessed | tf_op | source)
XLA Modules:
  0.0 319.2 jit_solution(4263212515151198260)
XLA Ops:
  7.2 0.0 copy-start
  7.2 0.0 all-reduce.7.cloned.1.call-start
  7.2 1.2 copy-done
  8.4 0.0 copy-start.4
  8.4 2.1 fusion.3
  10.5 0.0 copy-done.4
  10.6 0.0 copy-start.5
  10.6 0.8 fusion.2
  11.3 0.3 copy-done.5
  11.6 1.3 fusion.16
  12.9 0.0 all-reduce.7.cloned.1.call-update
  12.9 0.0 all-reduce.9.cloned.1.call-start
  12.9 36.2 %all-reduce.7.cloned.1.call-done = f32[512,256]{1,0:T(8,128)} async-done(((f32[512,256]{1,0:T(8,128)}), f32[512,256]{1,0:T(8,128)}) %all-reduce.7.cloned.1.call-update) | async-done | bytes 524304 | tf_op jit(solution)/shard_map/psum | solution.py:32
  49.2 1.5 fusion.10
  50.7 0.0 copy-done.3
  50.7 73.1 %all-reduce.12 = bf16[1024,256]{1,0:T(8,128)(2,1)} all-reduce(f32[1024,256]{1,0:T(8,128)S(1)} %fusion.10), channel_id=1, replica_groups=mesh['dp'=4,'center'=8] {'center'}, use_global_device_ids=true, to_apply=%region_3.0 | all-reduce | flops 262144 | bytes 1572864 | tf_op jit(solution)/shard_map/psum | solution.py:47
  123.8 2.5 fusion.8
  126.3 0.0 all-reduce.9.cloned.1.call-update
  126.4 0.0 all-reduce.11.cloned.1.call-start
  126.4 30.8 %all-reduce.9.cloned.1.call-done = f32[512,256]{1,0:T(8,128)} async-done(((f32[512,256]{1,0:T(8,128)}), f32[512,256]{1,0:T(8,128)}) %all-reduce.9.cloned.1.call-update) | async-done | bytes 524304 | tf_op jit(solution)/shard_map/psum | solution.py:32
  157.2 0.0 copy-done.1
  157.2 1.2 multiply_reduce_fusion.2
  158.4 21.4 %all-reduce = (f32[256]{0:T(256)S(1)}, f32[256]{0:T(256)S(1)}, f32[256]{0:T(256)S(1)}) all-reduce(f32[256]{0:T(256)S(1)} %get-tuple-element.4, f32[256]{0:T(256)S(1)} %get-tuple-element.3, f32[256]{0:T(256)S(1)} %get-tuple-element.2), channel_id=1, replica_groups=mesh['dp'=4,'center'=8] {'center'}, use_global_device_ids=true, to_apply=%region_2.0 | all-reduce | flops 768 | bytes 6144 | tf_op jit(solution)/shard_map/psum | solution.py:36
  179.8 1.8 fusion.11
  181.6 69.3 %all-reduce.13 = bf16[1024,256]{1,0:T(8,128)(2,1)} all-reduce(f32[1024,256]{1,0:T(8,128)S(1)} %fusion.11), channel_id=1, replica_groups=mesh['dp'=4,'center'=8] {'center'}, use_global_device_ids=true, to_apply=%region_9.0 | all-reduce | flops 262144 | bytes 1572864 | tf_op jit(solution)/shard_map/psum | solution.py:47
  250.8 2.5 fusion.6
  253.4 0.0 all-reduce.11.cloned.1.call-update
  253.4 34.3 %all-reduce.11.cloned.1.call-done = f32[512,256]{1,0:T(8,128)} async-done(((f32[512,256]{1,0:T(8,128)}), f32[512,256]{1,0:T(8,128)}) %all-reduce.11.cloned.1.call-update) | async-done | bytes 524304 | tf_op jit(solution)/shard_map/psum | solution.py:32
  287.7 0.0 copy-done.2
  287.7 1.3 multiply_reduce_fusion
  289.0 21.4 %psum.74 = f32[256]{0:T(256)S(1)} all-reduce(f32[256]{0:T(256)S(1)} %multiply_reduce_fusion), channel_id=1, replica_groups=mesh['dp'=4,'center'=8] {'center'}, use_global_device_ids=true, to_apply=%region_12.0 | all-reduce | flops 256 | bytes 2048 | tf_op jit(solution)/shard_map/psum | solution.py:36
  310.3 2.3 multiply_subtract_fusion
  (6 shorter events, 0.0 us)
Async XLA Ops:
  7.2 1.2 copy-start
  7.2 42.0 %all-reduce.7.cloned.1.call-start = ((), (), s32[]{:S(2)}) async-start(), calls=%async_computation | async-start | bytes 1048576 | tf_op jit(solution)/shard_map/psum | solution.py:32
  8.4 2.1 copy-start.4
  10.6 1.0 copy-start.5
  11.6 39.1 %copy-start.3 = (bf16[512,512]{1,0:T(8,128)(2,1)}, bf16[512,512]{1,0:T(8,128)(2,1)S(1)}, u32[]{:S(2)}) copy-start(bf16[512,512]{1,0:T(8,128)(2,1)S(1)} %fusion.2) | copy-start | bytes 1572868
  12.9 144.3 %all-reduce.9.cloned.1.call-start = ((), (), s32[]{:S(2)}) async-start(), calls=%async_computation.1 | async-start | bytes 1048576 | tf_op jit(solution)/shard_map/psum | solution.py:32
  123.8 33.4 %copy-start.1 = (f32[512,256]{1,0:T(8,128)S(1)}, f32[512,256]{1,0:T(8,128)}, u32[]{:S(2)}) copy-start(f32[512,256]{1,0:T(8,128)} %all-reduce.7.cloned.1.call-done) | copy-start | bytes 1572868
  126.4 161.3 %all-reduce.11.cloned.1.call-start = ((), (), s32[]{:S(2)}) async-start(), calls=%async_computation.2 | async-start | bytes 1048576 | tf_op jit(solution)/shard_map/psum | solution.py:32
  250.8 36.9 %copy-start.2 = (f32[512,256]{1,0:T(8,128)S(1)}, f32[512,256]{1,0:T(8,128)}, u32[]{:S(2)}) copy-start(f32[512,256]{1,0:T(8,128)} %all-reduce.9.cloned.1.call-done) | copy-start | bytes 1572868
Sparse Core Ops, SparseCore 0:
  13.0 36.1 all-reduce.6
  126.5 30.6 all-reduce.8
  253.5 34.1 all-reduce.10
where the time goes:
time: 320 us; the launch traced here: 319 us
  blocking collectives  185 us (58%)
  waiting for transfers between devices  101 us (32%)
  between operations  13.8 us (4%)
  matrix products  12.5 us (4%)
  other arithmetic  4.82 us (2%)
    psum x2, blocking collectives, apply_operator(): predicted = lax.psum(partial_value, 'center').astype(jnp.bfloat16)  142 us
    psum x3, waiting for transfers between devices, transposed_sum(): return lax.psum(local, 'dp')  101 us
    psum x2, blocking collectives, column_sums(): return lax.psum(values, 'center')  42.7 us
  transfers between devices with their start and end apart: 3, of which 3 were waited for; matrix products, arithmetic and copies ran while one was open for 0% of the time, Pallas kernels for 0%

commit v1 on v0

--- a/solution.py
+++ b/solution.py
@@ -29,7 +29,7 @@
     local = lax.dot_general(
         kernel, values, (((0,), (0,)), ((), ())), preferred_element_type=jnp.float32
     )
-    return lax.psum(local, "dp")
+    return jnp.sum(lax.all_gather(local, "dp"), axis=0)
 
 
 def column_sums(values):

time: 320 us -> 289 us (0.903)
  waiting for transfers between devices: 101 us -> 67.9 us
    psum x3 -> x0, waiting for transfers between devices: 101 us -> none  [transposed_sum(): return lax.psum(local, 'dp')]
    all_gather x0 -> x3, waiting for transfers between devices: none -> 67.8 us  [transposed_sum(): return jnp.sum(lax.all_gather(local, 'dp'), axis=0)]
    reduce_sum x0 -> x3, other arithmetic: none -> 5.36 us  [transposed_sum(): return jnp.sum(lax.all_gather(local, 'dp'), axis=0)]
where the time goes in v1:
time: 289 us
  blocking collectives  185 us (64%)
  waiting for transfers between devices  67.9 us (23%)
  between operations  13.8 us (5%)
  matrix products  12.5 us (4%)
  other arithmetic  7.06 us (2%)
    psum x2, blocking collectives, apply_operator(): predicted = lax.psum(partial_value, 'center').astype(jnp.bfloat16)  143 us
    all_gather x3, waiting for transfers between devices, transposed_sum(): return jnp.sum(lax.all_gather(local, 'dp'), axis=0)  67.8 us
    psum x2, blocking collectives, column_sums(): return lax.psum(values, 'center')  42.7 us
    dot_general x3, matrix products, transposed_sum(): lax.dot_general(kernel, values, (((0,), (0,)), ((), ())), preferred_eleme...  6.4 us
  transfers between devices with their start and end apart: 3, of which 3 were waited for; matrix products, arithmetic and copies ran while one was open for 0% of the time, Pallas kernels for 0%

profile of v1, /device:TPU:0, one launch (start us, length us, event | category | flops | bytes accessed | tf_op | source)
XLA Modules:
  0.0 288.7 jit_solution(18171134011448739615)
XLA Ops:
  7.2 0.0 copy-start
  7.2 0.0 all-gather.7.cloned.1.call-start
  7.2 1.2 copy-done
  8.4 2.1 fusion.3
  10.5 0.0 copy-done.3
  10.6 0.0 copy-start.4
  10.6 0.8 fusion.2
  11.3 0.0 copy-start.2
  11.4 0.8 copy-done.2
  12.1 1.3 fusion.16
  13.4 0.0 all-gather.7.cloned.1.call-update
  13.4 0.0 all-gather.9.cloned.1.call-start
  13.5 25.4 %all-gather.7.cloned.1.call-done = f32[2048,256]{1,0:T(8,128)} async-done(((f32[512,256]{1,0:T(8,128)}), f32[2048,256]{1,0:T(8,128)}) %all-gather.7.cloned.1.call-update) | async-done | bytes 2097168 | tf_op jit(solution)/shard_map/all_gather | solution.py:32
  38.9 1.8 reduce_sum.67
  40.7 1.5 fusion.10
  42.1 72.9 %all-reduce.3 = bf16[1024,256]{1,0:T(8,128)(2,1)} all-reduce(f32[1024,256]{1,0:T(8,128)S(1)} %fusion.10), channel_id=1, replica_groups=mesh['dp'=4,'center'=8] {'center'}, use_global_device_ids=true, to_apply=%region_3.0 | all-reduce | flops 262144 | bytes 1572864 | tf_op jit(solution)/shard_map/psum | solution.py:47
  115.1 2.5 fusion.8
  117.6 0.0 all-gather.9.cloned.1.call-update
  117.6 0.0 all-gather.11.cloned.1.call-start
  117.6 19.9 %all-gather.9.cloned.1.call-done = f32[2048,256]{1,0:T(8,128)} async-done(((f32[512,256]{1,0:T(8,128)}), f32[2048,256]{1,0:T(8,128)}) %all-gather.9.cloned.1.call-update) | async-done | bytes 2097168 | tf_op jit(solution)/shard_map/all_gather | solution.py:32
  137.5 1.8 reduce_sum.69
  139.3 0.2 multiply_reduce_fusion.2
  139.5 21.4 %all-reduce = (f32[256]{0:T(256)S(1)}, f32[256]{0:T(256)S(1)}, f32[256]{0:T(256)S(1)}) all-reduce(f32[256]{0:T(256)S(1)} %get-tuple-element.4, f32[256]{0:T(256)S(1)} %get-tuple-element.3, f32[256]{0:T(256)S(1)} %get-tuple-element.2), channel_id=1, replica_groups=mesh['dp'=4,'center'=8] {'center'}, use_global_device_ids=true, to_apply=%region_2.0 | all-reduce | flops 768 | bytes 6144 | tf_op jit(solution)/shard_map/psum | solution.py:36
  160.9 1.7 fusion.11
  162.7 69.6 %all-reduce.4 = bf16[1024,256]{1,0:T(8,128)(2,1)} all-reduce(f32[1024,256]{1,0:T(8,128)S(1)} %fusion.11), channel_id=1, replica_groups=mesh['dp'=4,'center'=8] {'center'}, use_global_device_ids=true, to_apply=%region_9.0 | all-reduce | flops 262144 | bytes 1572864 | tf_op jit(solution)/shard_map/psum | solution.py:47
  232.3 2.6 fusion.6
  234.9 0.0 all-gather.11.cloned.1.call-update
  234.9 22.5 %all-gather.11.cloned.1.call-done = f32[2048,256]{1,0:T(8,128)} async-done(((f32[512,256]{1,0:T(8,128)}), f32[2048,256]{1,0:T(8,128)}) %all-gather.11.cloned.1.call-update) | async-done | bytes 2097168 | tf_op jit(solution)/shard_map/all_gather | solution.py:32
  257.5 1.8 reduce_sum.72
  259.3 0.2 multiply_reduce_fusion
  259.5 21.4 %psum.50 = f32[256]{0:T(256)S(1)} all-reduce(f32[256]{0:T(256)S(1)} %multiply_reduce_fusion), channel_id=1, replica_groups=mesh['dp'=4,'center'=8] {'center'}, use_global_device_ids=true, to_apply=%region_12.0 | all-reduce | flops 256 | bytes 2048 | tf_op jit(solution)/shard_map/psum | solution.py:36
  280.9 1.2 multiply_subtract_fusion
  (7 shorter events, 0.0 us)
Async XLA Ops:
  7.2 1.2 copy-start
  7.2 31.7 %all-gather.7.cloned.1.call-start = ((), (), s32[]{:S(2)}) async-start(), calls=%async_computation | async-start | bytes 2621440 | tf_op jit(solution)/shard_map/all_gather | solution.py:32
  8.4 2.1 copy-start.3
  10.6 104.5 %copy-start.1 = (bf16[512,512]{1,0:T(8,128)(2,1)}, bf16[512,512]{1,0:T(8,128)(2,1)S(1)}, u32[]{:S(2)}) copy-start(bf16[512,512]{1,0:T(8,128)(2,1)S(1)} %fusion.3) | copy-start | bytes 1572868
  10.6 1.6 copy-start.4
  11.3 0.8 copy-start.2
  13.4 124.1 %all-gather.9.cloned.1.call-start = ((), (), s32[]{:S(2)}) async-start(), calls=%async_computation.1 | async-start | bytes 2621440 | tf_op jit(solution)/shard_map/all_gather | solution.py:32
  117.6 139.9 %all-gather.11.cloned.1.call-start = ((), (), s32[]{:S(2)}) async-start(), calls=%async_computation.2 | async-start | bytes 2621440 | tf_op jit(solution)/shard_map/all_gather | solution.py:32
Sparse Core Ops, SparseCore 0:
  13.6 25.2 all-gather.6
  117.7 19.7 all-gather.8
  235.0 22.3 all-gather.10
